TPU v7x, 32 devices: a whole 2x2x4 slice. The times are simulated.
32 devices in a mesh: tm: 4 (over y, x), space: 8 (over z, core).
Axes of the slice: x: 2, y: 2, z: 4, core: 2. Of those that a mesh axis runs over, the one named last changes fastest.
Arguments:
- source: float32 [8, 1024, 5, 128], P('tm', 'space'), may hold values from -6 to 6
- terminal: float32 [1024, 5, 128], P('space'), may hold values from -6 to 6
- jacobian: float32 [4, 1024, 5, 5, 128], P('tm', 'space')
- face_coef: float32 [1024, 6, 128], P('space'), may hold values from 0.1 to 0.5
- cell_coef: float32 [1024, 128], P('space'), may hold values from 0.1 to 0.5
- neighbours: int32 [1024, 6], P('space'), may hold values from 0 to 160, as said below
- send_blocks: int32 [8, 2, 16], P('space'), may hold values from 0 to 127, as said below
- live_count: int32 [8], P('space'), may hold values from 64 to 128, as said below
- volume: float32 [1024, 128], P('space'), may hold values from 0.5 to 2
- shape_field: float32 [1024, 5, 128], P('space'), may hold values from -6 to 6
- weights: float32 [8], P('tm'), may hold values from 0.25 to 4
Outputs:
- adjoint: float32 [8, 1024, 5, 128], P('tm', 'space')
- sensitivity: float32 [1024], P('space')
Inputs may be any that keep to these rules, and one draw needn't show every extreme that they name: `live_count`: some device has 128 live blocks in every draw. `send_blocks`: each index names a live block of its own device. `neighbours`: a slot below 128 names a live block of the same device; 128 to 159 name received blocks, those of the lower device first; 160 is an empty slot.
All inputs are finite; a program needn't handle non-finite values.
Results may differ from a plain program's by a relative error of at most 0.00016.
Values sent between devices are 32-bit elements; how exact they have to be, the bound alone decides.
A program may use at most 64 MiB of HBM per device.

v0:
```python
import functools

import jax
import jax.numpy as jnp
from jax import lax
from jax.experimental import pallas as pl
from jax.experimental.pallas import tpu as pltpu
from jax.sharding import PartitionSpec as P

ITERS = 3
INVERSE_STEP = 6.0
TILE = 16
HIGHEST = lax.Precision.HIGHEST


def rows_at(start):
    return pl.ds(start if isinstance(start, int) else pl.multiple_of(start, TILE), TILE)


def split(x):
    high = x.astype(jnp.bfloat16)
    return high, (x - high.astype(jnp.float32)).astype(jnp.bfloat16)


def matmul(a, b, precision=None):
    return jnp.dot(a, b, precision=precision, preferred_element_type=jnp.float32)


def kernel(
    groups,
    width,
    source_hbm,
    terminal_hbm,
    jac_hbm,
    face_hbm,
    cell_hbm,
    nbr_hbm,
    send_blocks,
    live_count,
    volume_hbm,
    shape_hbm,
    weights,
    adjoint_hbm,
    sens_ref,
    source,
    terminal,
    jac,
    face,
    cell,
    nbr,
    volume,
    shape,
    field,
    part,
    rate,
    rate_mass,
    cell_left,
    cell_right,
    rhs,
    levels,
    weighted,
    near_pick,
    far_pick,
    field_terms,
    part_terms,
    halo_terms,
    near,
    far,
    select,
    select_terms,
    edge_pick,
    edge_face,
    edge_rate,
    edge_part,
    halo,
    outbox,
    acc_in,
    acc_out,
    total,
    load_sem,
    store_sem,
    halo_send,
    halo_recv,
    state_send,
    state_recv,
    acc_send,
    acc_recv,
    total_send,
    total_recv,
):
    g = lax.axis_index("tm")
    d = lax.axis_index("space")
    steps, comp, nb, cells = source.shape
    nei = face.shape[0]
    count = outbox.shape[3]
    sweeps = steps * ITERS
    tiles = nb // TILE
    edges = 2 * count
    chunks = [(a, min(a + 2, comp)) for a in range(0, comp, 2)]

    loads = [
        pltpu.make_async_copy(nbr_hbm, nbr, load_sem.at[0]),
        pltpu.make_async_copy(face_hbm, face, load_sem.at[1]),
        pltpu.make_async_copy(cell_hbm, cell, load_sem.at[2]),
        pltpu.make_async_copy(volume_hbm, volume, load_sem.at[3]),
        pltpu.make_async_copy(jac_hbm.at[0], jac, load_sem.at[4]),
        pltpu.make_async_copy(terminal_hbm, terminal, load_sem.at[5]),
        pltpu.make_async_copy(source_hbm, source, load_sem.at[6]),
        pltpu.make_async_copy(shape_hbm, shape, load_sem.at[7]),
    ]
    for load in loads:
        load.start()

    @pl.when((d == 0) | (d == width - 1))
    def _():
        halo[...] = jnp.zeros_like(halo)

    barrier = pltpu.get_barrier_semaphore()
    for other in range(groups):
        @pl.when(g != other)
        def _():
            pl.semaphore_signal(barrier, inc=1, device_id={"tm": other})

    def greet(side):
        pl.semaphore_signal(barrier, inc=1, device_id={"space": side})

        @pl.when(g > 0)
        def _():
            pl.semaphore_signal(barrier, inc=1, device_id={"tm": g - 1, "space": side})

        @pl.when(g < groups - 1)
        def _():
            pl.semaphore_signal(barrier, inc=1, device_id={"tm": g + 1, "space": side})

    @pl.when(d > 0)
    def _():
        greet(d - 1)

    @pl.when(d < width - 1)
    def _():
        greet(d + 1)

    halo_terms[...] = jnp.zeros_like(halo_terms)
    lane = lax.broadcasted_iota(jnp.int32, (1, nb), 1)
    for side in range(2):
        for s in range(count):
            row = side * count + s
            select[pl.ds(row, 1), :] = jnp.where(lane == send_blocks[0, side, s], 1.0, 0.0)
    chosen = select[...]
    chosen_low = chosen.astype(jnp.bfloat16)
    select_terms[:, :nb] = chosen_low
    select_terms[:, nb:] = chosen_low

    loads[0].wait()
    listed = nbr[...].astype(jnp.float32)
    listed = jnp.concatenate([listed, jnp.zeros((nb - nei, nb), jnp.float32)], axis=0).T
    wide = lax.broadcasted_iota(jnp.int32, (nb, nb), 1).astype(jnp.float32)
    for k in range(nei):
        column = jnp.broadcast_to(listed[:, k : k + 1], (nb, nb))
        pick = jnp.where(column == wide, 1.0, 0.0).astype(jnp.bfloat16)
        near_pick[pl.ds(k * nb, nb), :nb] = pick
        near_pick[pl.ds(k * nb, nb), nb:] = pick
        outer = column - nb
        hit = (outer == wide) | (outer + edges == wide)
        inside = (outer >= 0) & (outer < edges)
        pick = jnp.where(hit & inside, 1.0, 0.0).astype(jnp.bfloat16)
        far_pick[pl.ds(k * nb, nb), :] = pick
        edge_pick[pl.ds(k * edges, edges), :] = matmul(chosen_low, pick).astype(jnp.bfloat16)

    for load in loads[1:5]:
        load.wait()
    alive = live_count[0]
    row_id = lax.broadcasted_iota(jnp.int32, (TILE, cells), 0)
    lane_id = lax.broadcasted_iota(jnp.int32, (TILE, cells), 1)

    def live_of(t):
        return jnp.where(row_id + t * TILE < alive, 1.0, 0.0)

    def prepare(t, _):
        r = rows_at(t * TILE)
        live = live_of(t)
        mass = INVERSE_STEP * volume[r, :]
        along = cell[r, :]
        base = mass + 2.0 * along
        for k in range(nei):
            base = base + face[k, r, :]
        cell_left[r, :] = jnp.where(lane_id == 0, 0.0, along)
        cell_right[r, :] = jnp.where(lane_id == cells - 1, 0.0, along)
        for j in range(comp):
            c = live / (base + jac[j, j, r, :])
            rate[j, r, :] = c
            drift = c * mass
            rate_mass[j, r, :] = drift
            for i in range(comp):
                entry = -c * jac[i, j, r, :]
                jac[i, j, r, :] = entry + (live - drift) if i == j else entry
            weighted[j, r, :] = jnp.zeros((TILE, cells), jnp.float32)
        return 0

    for t in range(tiles):
        prepare(t, 0)
    for k in range(nei):
        edge_face[k] = matmul(chosen, face[k], HIGHEST)
    for j in range(comp):
        edge_rate[j] = matmul(chosen, rate[j], HIGHEST)

    for load in loads[5:]:
        load.wait()
    sides = jnp.where(d > 0, 1, 0) + jnp.where(d < width - 1, 1, 0)
    slabs = 1 + jnp.where(g > 0, 1, 0) + jnp.where(g < groups - 1, 1, 0)
    pl.semaphore_wait(barrier, groups - 1 + sides * slabs)

    def lanes(j):
        return slice(j * cells, (j + 1) * cells)

    def put_terms(ref, t, j, x):
        high, low = split(x)
        ref[rows_at(t * TILE), lanes(j)] = high
        ref[rows_at(nb + t * TILE), lanes(j)] = low

    def state_copy(to):
        return pltpu.make_async_remote_copy(
            src_ref=field, dst_ref=field, send_sem=state_send, recv_sem=state_recv,
            device_id={"tm": to},
        )

    @pl.when(g == groups - 1)
    def _():
        def begin(t, _):
            r = rows_at(t * TILE)
            for j in range(comp):
                field[j, r, :] = live_of(t) * terminal[j, r, :]
            return 0

        for t in range(tiles):
            begin(t, 0)

    @pl.when(g < groups - 1)
    def _():
        state_copy(g).wait_recv()

    def begin_terms(t, _):
        r = rows_at(t * TILE)
        for j in range(comp):
            put_terms(field_terms, t, j, field[j, r, :])
        return 0

    for t in range(tiles):
        begin_terms(t, 0)

    def halo_copy(slot, side, c, to):
        own = slot < sweeps
        first, last = chunks[c]
        part_of = pl.ds(first, last - first)
        place = jnp.where(own, slot, 0)
        return pltpu.make_async_remote_copy(
            src_ref=outbox.at[slot, side, part_of],
            dst_ref=halo.at[place, 1 - side, part_of],
            send_sem=halo_send.at[slot, side, c],
            recv_sem=halo_recv.at[place, 1 - side, c],
            device_id={"tm": jnp.where(own, g, g - 1), "space": to},
        )

    def send(slot, c):
        wanted = (slot < sweeps) | (g > 0)

        @pl.when((d > 0) & wanted)
        def _():
            halo_copy(slot, 0, c, d - 1).start()

        @pl.when((d < width - 1) & wanted)
        def _():
            halo_copy(slot, 1, c, d + 1).start()

    def receive(m, c):
        @pl.when(d > 0)
        def _():
            halo_copy(m, 1, c, d - 1).wait_recv()

        @pl.when(d < width - 1)
        def _():
            halo_copy(m, 0, c, d + 1).wait_recv()

    @pl.when(g == groups - 1)
    def _():
        first_out = matmul(select_terms[...], field_terms[...])
        for side in range(2):
            for j in range(comp):
                outbox[0, side, j] = first_out[side * count : (side + 1) * count, lanes(j)]
        for c in range(len(chunks)):
            send(0, c)

    def sweep(m):
        near[...] = matmul(near_pick[...], field_terms[...])

        def local(t, _):
            r = rows_at(t * TILE)
            x = [field[i, r, :] for i in range(comp)]
            left = cell_left[r, :]
            right = cell_right[r, :]
            for j in range(comp):
                value = left * pltpu.roll(x[j], 1, 1) + right * pltpu.roll(x[j], cells - 1, 1)
                for k in range(nei):
                    q = rows_at(k * nb + t * TILE)
                    value = value + face[k, r, :] * near[q, lanes(j)]
                value = rhs[j, r, :] + rate[j, r, :] * value
                for i in range(comp):
                    value = value + jac[i, j, r, :] * x[i]
                part[j, r, :] = value
                put_terms(part_terms, t, j, value)
            return 0

        for t in range(tiles):
            local(t, 0)
        edge_part[...] = matmul(select_terms[...], part_terms[...])
        for c, (first, last) in enumerate(chunks):
            receive(m, c)
            for side in range(2):
                low_rows = slice(edges + side * count, edges + (side + 1) * count)
                for j in range(first, last):
                    high, low = split(halo[m, side, j])
                    halo_terms[side * count : (side + 1) * count, lanes(j)] = high
                    halo_terms[low_rows, lanes(j)] = low
            arrived = matmul(edge_pick[...], halo_terms[:, first * cells : last * cells])
            for side in range(2):
                rows = slice(side * count, (side + 1) * count)
                for j in range(first, last):
                    value = None
                    for k in range(nei):
                        q = slice(k * edges + side * count, k * edges + (side + 1) * count)
                        term = edge_face[k, rows, :] * arrived[q, lanes(j - first)]
                        value = term if value is None else value + term
                    outbox[m + 1, side, j] = edge_part[rows, lanes(j)] + edge_rate[j, rows, :] * value
            send(m + 1, c)

        far[...] = matmul(far_pick[...], halo_terms[...])

        def bulk(t, _):
            r = rows_at(t * TILE)
            for j in range(comp):
                value = None
                for k in range(nei):
                    q = rows_at(k * nb + t * TILE)
                    term = face[k, r, :] * far[q, lanes(j)]
                    value = term if value is None else value + term
                value = part[j, r, :] + rate[j, r, :] * value
                field[j, r, :] = value
                put_terms(field_terms, t, j, value)
            return 0

        for t in range(tiles):
            bulk(t, 0)

    def level_copy(n):
        return pltpu.make_async_copy(levels.at[n], adjoint_hbm.at[n], store_sem.at[n])

    def level(step, _):
        n = steps - 1 - step

        def start(t, _):
            r = rows_at(t * TILE)
            for j in range(comp):
                rhs[j, r, :] = rate[j, r, :] * source[n, j, r, :] + rate_mass[j, r, :] * field[j, r, :]
            return 0

        for t in range(tiles):
            start(t, 0)

        def inner(it, _):
            sweep(step * ITERS + it)
            return 0

        lax.fori_loop(0, ITERS, inner, 0)

        @pl.when((step == steps - 1) & (g > 0))
        def _():
            state_copy(g - 1).start()

        weight = weights[n]

        def finish(t, _):
            r = rows_at(t * TILE)
            for j in range(comp):
                x = field[j, r, :]
                levels[n, j, r, :] = x
                weighted[j, r, :] = weighted[j, r, :] + weight * x
            return 0

        for t in range(tiles):
            finish(t, 0)
        level_copy(n).start()
        return 0

    lax.fori_loop(0, steps, level, 0)

    summed = jnp.zeros((nb, cells), jnp.float32)
    for j in range(comp):
        summed = summed + weighted[j] * shape[j]

    mine = lax.dot_general(
        jnp.ones((8, cells), jnp.float32),
        summed,
        (((1,), (1,)), ((), ())),
        precision=lax.Precision.HIGHEST,
        preferred_element_type=jnp.float32,
    )

    def acc_copy(to):
        return pltpu.make_async_remote_copy(
            src_ref=acc_out, dst_ref=acc_in, send_sem=acc_send, recv_sem=acc_recv,
            device_id={"tm": to},
        )

    def total_copy(to):
        return pltpu.make_async_remote_copy(
            src_ref=acc_out, dst_ref=total, send_sem=total_send.at[to], recv_sem=total_recv,
            device_id={"tm": to},
        )

    @pl.when(g == groups - 1)
    def _():
        acc_out[...] = mine

    @pl.when(g < groups - 1)
    def _():
        acc_copy(g).wait_recv()
        acc_out[...] = mine + acc_in[...]

    @pl.when(g > 0)
    def _():
        acc_copy(g - 1).start()
        total_copy(g).wait_recv()
        sens_ref[...] = total[0:1, :]

    @pl.when(g == 0)
    def _():
        for other in range(1, groups):
            total_copy(other).start()
        sens_ref[...] = acc_out[0:1, :]
        for other in range(1, groups):
            total_copy(other).wait_send()

    @pl.when(g > 0)
    def _():
        acc_copy(g - 1).wait_send()
        state_copy(g - 1).wait_send()

    def drain(slot, _):
        wanted = ((slot > 0) | (g == groups - 1)) & ((slot < sweeps) | (g > 0))
        for c in range(len(chunks)):
            @pl.when((d > 0) & wanted)
            def _():
                halo_copy(slot, 0, c, d - 1).wait_send()

            @pl.when((d < width - 1) & wanted)
            def _():
                halo_copy(slot, 1, c, d + 1).wait_send()

        return 0

    lax.fori_loop(0, sweeps + 1, drain, 0)
    for n in range(steps):
        level_copy(n).wait()


def per_device(groups, width, *args):
    (source, terminal, jacobian, face_coef, cell_coef, neighbours, send_blocks,
     live_count, volume, shape_field, weights) = args
    steps, nb, comp, cells = source.shape
    nei = face_coef.shape[1]
    count = send_blocks.shape[2]
    edges = 2 * count
    sweeps = steps * ITERS
    f32 = jnp.float32
    bf16 = jnp.bfloat16
    hbm = pl.BlockSpec(memory_space=pltpu.MemorySpace.HBM)
    smem = pl.BlockSpec(memory_space=pltpu.SMEM)
    vmem = pltpu.VMEM
    dma = pltpu.SemaphoreType.DMA
    block = (comp, nb, cells)
    flat = comp * cells
    chunks = -(-comp // 2)
    adjoint, sens = pl.pallas_call(
        functools.partial(kernel, groups, width),
        out_shape=(
            jax.ShapeDtypeStruct((steps, comp, nb, cells), f32),
            jax.ShapeDtypeStruct((1, nb), f32),
        ),
        in_specs=[hbm, hbm, hbm, hbm, hbm, hbm, smem, smem, hbm, hbm, smem],
        out_specs=(hbm, pl.BlockSpec(memory_space=pltpu.VMEM)),
        scratch_shapes=[
            vmem((steps, comp, nb, cells), f32),
            vmem(block, f32),
            vmem((comp, comp, nb, cells), f32),
            vmem((nei, nb, cells), f32),
            vmem((nb, cells), f32),
            vmem((nei, nb), jnp.int32),
            vmem((nb, cells), f32),
            vmem(block, f32),
            vmem(block, f32),
            vmem(block, f32),
            vmem(block, f32),
            vmem(block, f32),
            vmem((nb, cells), f32),
            vmem((nb, cells), f32),
            vmem(block, f32),
            vmem((steps, comp, nb, cells), f32),
            vmem(block, f32),
            vmem((nei * nb, 2 * nb), bf16),
            vmem((nei * nb, nb), bf16),
            vmem((2 * nb, flat), bf16),
            vmem((2 * nb, flat), bf16),
            vmem((nb, flat), bf16),
            vmem((nei * nb, flat), f32),
            vmem((nei * nb, flat), f32),
            vmem((edges, nb), f32),
            vmem((edges, 2 * nb), bf16),
            vmem((nei * edges, nb), bf16),
            vmem((nei, edges, cells), f32),
            vmem((comp, edges, cells), f32),
            vmem((edges, flat), f32),
            vmem((sweeps, 2, comp, count, cells), f32),
            vmem((sweeps + 1, 2, comp, count, cells), f32),
            vmem((8, nb), f32),
            vmem((8, nb), f32),
            vmem((8, nb), f32),
            dma((8,)),
            dma((steps,)),
            dma((sweeps + 1, 2, chunks)),
            dma((sweeps, 2, chunks)),
            dma,
            dma,
            dma,
            dma,
            dma((groups,)),
            dma,
        ],
        compiler_params=pltpu.CompilerParams(collective_id=0, has_side_effects=True),
    )(
        source.transpose(0, 2, 1, 3),
        terminal.transpose(1, 0, 2),
        jacobian.transpose(0, 2, 3, 1, 4),
        face_coef.transpose(1, 0, 2),
        cell_coef,
        neighbours.T,
        send_blocks,
        live_count,
        volume,
        shape_field.transpose(1, 0, 2),
        weights,
    )
    return adjoint.transpose(0, 2, 1, 3), sens.reshape(nb)


def solution(mesh):
    sizes = dict(mesh.shape)
    return jax.shard_map(
        functools.partial(per_device, sizes["tm"], sizes["space"]),
        mesh=mesh,
        in_specs=(
            P("tm", "space", None, None),
            P("space", None, None),
            P("tm", "space", None, None, None),
            P("space", None, None),
            P("space", None),
            P("space", None),
            P("space", None, None),
            P("space"),
            P("space", None),
            P("space", None, None),
            P("tm"),
        ),
        out_specs=(P("tm", "space", None, None), P("space")),
        check_vma=False,
    )
```

profile of v0, /device:TPU:0, one launch (start us, length us, event | category | flops | bytes accessed | tf_op | source)
XLA Modules:
  0.0 101.4 jit_solution(6459686978901896086)
XLA Ops:
  1.3 97.0 %shard_map.122 = (f32[2,5,128,128]{3,2,1,0:T(8,128)}, f32[1,128]{1,0:T(1,128)}) custom-call(f32[2,5,128,128]{3,2,1,0:T(8,128)} %bitcast.10, f32[5,128,128]{2,1,0:T(8,128)} %bitcast.12, f32[1,5,5,128,128]{4,3,2,1,0:T(8,128)} %bitcast.8, f32[6,128,128]{2,1,0:T(8,128)} %bitcast.11, f32[128,128]{1,0:T(8,128)} %cell_hbm.1, s32[6,128]{1,0:T(8,128)} %bitcast.14, ...), custom_call_target="tpu_custom_call" | custom-call | tf_op jit(solution)/shard_map/pallas_call | solution.py:483
  98.2 2.0 %copy.16 = f32[2,128,5,128]{3,1,2,0:T(8,128)} copy(f32[2,128,5,128]{3,1,2,0:T(8,128)} %bitcast.9) | data formatting | bytes 1310720
  100.2 1.2 %copy.17 = f32[128]{0:T(128)} copy(f32[128]{0:T(128)} %bitcast.15) | data formatting | bytes 1024
where the time goes:
time: 103 us; the launch traced here: 101 us
  Pallas kernels  97 us (94%)
  local copies, waits for them, and re-layouts  3.14 us (3%)
  between operations  1.29 us (1%)
    pallas_call x1, Pallas kernels, per_device(): pl.pallas_call(functools.partial(kernel, groups, width), out_shape=(jax.S...  97 us
    unnamed x2, local copies, waits for them, and re-layouts  3.14 us

commit v1 on v0

v1 whole, which is shorter than its diff:
```python
import functools

import jax
import jax.numpy as jnp
from jax import lax
from jax.experimental import pallas as pl
from jax.experimental.pallas import tpu as pltpu
from jax.sharding import PartitionSpec as P

ITERS = 3
INVERSE_STEP = 6.0
TILE = 16
HIGHEST = lax.Precision.HIGHEST


def rows_at(start):
    return pl.ds(start if isinstance(start, int) else pl.multiple_of(start, TILE), TILE)


def split(x):
    high = x.astype(jnp.bfloat16)
    return high, (x - high.astype(jnp.float32)).astype(jnp.bfloat16)


def matmul(a, b, precision=None):
    return jnp.dot(a, b, precision=precision, preferred_element_type=jnp.float32)


def kernel(
    groups,
    width,
    source_hbm,
    terminal_hbm,
    jac_hbm,
    face_hbm,
    cell_hbm,
    nbr_hbm,
    send_blocks,
    live_count,
    volume_hbm,
    shape_hbm,
    weights,
    adjoint_hbm,
    sens_ref,
    source,
    terminal,
    jac,
    face,
    cell,
    nbr,
    volume,
    shape,
    field,
    part,
    rate,
    rate_mass,
    cell_left,
    cell_right,
    rhs,
    levels,
    weighted,
    near_pick,
    far_pick,
    field_terms,
    part_terms,
    halo_terms,
    edge_terms,
    near,
    far,
    select,
    select_terms,
    own_fixed,
    own_rate,
    their_fixed,
    their_rate,
    their_pick,
    edge_halo,
    from_partner,
    from_across,
    from_second,
    edge_out,
    part_out,
    acc_in,
    acc_out,
    total,
    load_sem,
    store_sem,
    copy_send,
    copy_recv,
    coef_send,
    coef_recv,
    partner_send,
    partner_recv,
    across_send,
    across_recv,
    second_send,
    second_recv,
    first_send,
    state_send,
    state_recv,
    acc_send,
    acc_recv,
    total_send,
    total_recv,
):
    g = lax.axis_index("tm")
    d = lax.axis_index("space")
    _, steps, comp, nb, cells = source.shape
    nei = face.shape[0]
    count = edge_out.shape[3]
    sweeps = steps * ITERS
    tiles = nb // TILE
    edges = 2 * count
    top = groups - 1

    odd = lax.rem(d, 2)
    partner = d + 1 - 2 * odd
    across = d - 1 + 2 * odd
    beyond = d + 2 - 4 * odd
    second = d - 2 + 4 * odd
    has_across = (across >= 0) & (across < width)
    has_beyond = (beyond >= 0) & (beyond < width)

    even = lax.rem(g, 2) == 0
    down_two = even & (g > 1)
    down_one = down_two | (g == top)
    copies = (lax.rem(g, 2) == 1) & (g < top)
    twice = (lax.rem(g, 2) == 0) & (g + 1 < top)
    stages = jnp.where(twice, 2, 1)
    last = stages * sweeps

    loads = [
        pltpu.make_async_copy(nbr_hbm, nbr, load_sem.at[0]),
        pltpu.make_async_copy(face_hbm, face, load_sem.at[1]),
        pltpu.make_async_copy(cell_hbm, cell, load_sem.at[2]),
        pltpu.make_async_copy(volume_hbm, volume, load_sem.at[3]),
        pltpu.make_async_copy(jac_hbm.at[0], jac.at[0], load_sem.at[4]),
        pltpu.make_async_copy(terminal_hbm, terminal, load_sem.at[5]),
        pltpu.make_async_copy(source_hbm, source.at[0], load_sem.at[6]),
        pltpu.make_async_copy(shape_hbm, shape, load_sem.at[7]),
    ]
    for load in loads:
        load.start()

    @pl.when(jnp.logical_not(has_across))
    def _():
        from_across[...] = jnp.zeros_like(from_across)

    barrier = pltpu.get_barrier_semaphore()
    for other in range(groups):
        @pl.when(g != other)
        def _():
            pl.semaphore_signal(barrier, inc=1, device_id={"tm": other})

    up_two = even & (g + 2 < groups)
    up_one = (jnp.logical_not(even) & (g + 1 < groups)) | (g + 1 == top)

    def greet(side):
        pl.semaphore_signal(barrier, inc=1, device_id={"space": side})
        for shift, linked in ((-2, down_two), (-1, down_one), (1, up_one), (2, up_two)):
            @pl.when(linked)
            def _():
                pl.semaphore_signal(barrier, inc=1, device_id={"tm": g + shift, "space": side})

    for shift in (1, 2):
        @pl.when(d > shift - 1)
        def _():
            greet(d - shift)

        @pl.when(d < width - shift)
        def _():
            greet(d + shift)

    sides = sum(jnp.where(d > i - 1, 1, 0) + jnp.where(d < width - i, 1, 0) for i in (1, 2))
    slabs = 1 + sum(jnp.where(linked, 1, 0) for linked in (down_two, down_one, up_one, up_two))
    expected = groups - 1 + sides * slabs

    def jac_copy(to):
        return pltpu.make_async_remote_copy(
            src_ref=jac_hbm.at[0], dst_ref=jac.at[1], send_sem=copy_send.at[0],
            recv_sem=copy_recv.at[0], device_id={"tm": to},
        )

    def source_copy(n, to):
        return pltpu.make_async_remote_copy(
            src_ref=source_hbm.at[n], dst_ref=source.at[1, n], send_sem=copy_send.at[1 + n],
            recv_sem=copy_recv.at[1 + n], device_id={"tm": to},
        )

    @pl.when(copies)
    def _():
        pl.semaphore_wait(barrier, expected)
        jac_copy(g - 1).start()
        for n in reversed(range(steps)):
            source_copy(n, g - 1).start()

    halo_terms[...] = jnp.zeros_like(halo_terms)
    edge_terms[...] = jnp.zeros_like(edge_terms)
    edge_halo[...] = jnp.zeros_like(edge_halo)
    lane = lax.broadcasted_iota(jnp.int32, (1, nb), 1)
    for i in range(2):
        for s in range(count):
            row = i * count + s
            block = jnp.where(odd == i, send_blocks[0, 1, s], send_blocks[0, 0, s])
            select[pl.ds(row, 1), :] = jnp.where(lane == block, 1.0, 0.0)
    chosen_low = select[...].astype(jnp.bfloat16)
    select_terms[:, :nb] = chosen_low
    select_terms[:, nb:] = chosen_low
    chosen = select[count:edges, :]
    chosen_low = chosen.astype(jnp.bfloat16)

    loads[0].wait()
    listed = nbr[...].astype(jnp.float32)
    listed = jnp.concatenate([listed, jnp.zeros((nb - nei, nb), jnp.float32)], axis=0).T
    wide = lax.broadcasted_iota(jnp.int32, (nb, nb), 1).astype(jnp.float32)
    swap = ((1 - odd) * count).astype(jnp.float32)
    for k in range(nei):
        column = jnp.broadcast_to(listed[:, k : k + 1], (nb, nb))
        pick = jnp.where(column == wide, 1.0, 0.0).astype(jnp.bfloat16)
        near_pick[pl.ds(k * nb, nb), :nb] = pick
        near_pick[pl.ds(k * nb, nb), nb:] = pick
        shifted = column - nb
        inside = (shifted >= 0) & (shifted < edges)
        shifted = shifted + swap * jnp.where(shifted < count, 1.0, -1.0)
        hit = (shifted == wide) | (shifted + edges == wide)
        pick = jnp.where(hit & inside, 1.0, 0.0).astype(jnp.bfloat16)
        far_pick[pl.ds(k * nb, nb), :] = pick
        own_fixed[k] = matmul(chosen_low, pick)

    for load in loads[1:5]:
        load.wait()
    alive = live_count[0]
    row_id = lax.broadcasted_iota(jnp.int32, (TILE, cells), 0)
    lane_id = lax.broadcasted_iota(jnp.int32, (TILE, cells), 1)

    def live_of(t):
        return jnp.where(row_id + t * TILE < alive, 1.0, 0.0)

    def prepare(t, store):
        r = rows_at(t * TILE)
        live = live_of(t)
        mass = INVERSE_STEP * volume[r, :]
        along = cell[r, :]
        base = mass + 2.0 * along
        for k in range(nei):
            base = base + face[k, r, :]
        if store == 0:
            cell_left[r, :] = jnp.where(lane_id == 0, 0.0, along)
            cell_right[r, :] = jnp.where(lane_id == cells - 1, 0.0, along)
        for j in range(comp):
            c = live / (base + jac[store, j, j, r, :])
            rate[store, j, r, :] = c
            drift = c * mass
            rate_mass[store, j, r, :] = drift
            for i in range(comp):
                entry = -c * jac[store, i, j, r, :]
                jac[store, i, j, r, :] = entry + (live - drift) if i == j else entry
            if store == 0:
                weighted[j, r, :] = jnp.zeros((TILE, cells), jnp.float32)

    def fixed_copy():
        return pltpu.make_async_remote_copy(
            src_ref=own_fixed, dst_ref=their_fixed, send_sem=coef_send.at[0],
            recv_sem=coef_recv.at[0], device_id={"space": across},
        )

    def rate_copy(store):
        return pltpu.make_async_remote_copy(
            src_ref=own_rate.at[store], dst_ref=their_rate.at[store], send_sem=coef_send.at[1 + store],
            recv_sem=coef_recv.at[1 + store], device_id={"space": across},
        )

    for t in range(tiles):
        prepare(t, 0)
    for k in range(nei):
        own_fixed[nei + k] = matmul(chosen, face[k], HIGHEST)
    for j in range(comp):
        own_rate[0, j] = matmul(chosen, rate[0, j], HIGHEST)

    for load in loads[5:]:
        load.wait()

    @pl.when(jnp.logical_not(copies))
    def _():
        pl.semaphore_wait(barrier, expected)

    def lanes(j):
        return slice(j * cells, (j + 1) * cells)

    def put_terms(ref, t, j, x):
        high, low = split(x)
        ref[rows_at(t * TILE), lanes(j)] = high
        ref[rows_at(nb + t * TILE), lanes(j)] = low

    def put_edges(ref, side, j, x):
        high, low = split(x)
        ref[side * count : (side + 1) * count, lanes(j)] = high
        ref[edges + side * count : edges + (side + 1) * count, lanes(j)] = low

    def state_copy(way, to):
        return pltpu.make_async_remote_copy(
            src_ref=field, dst_ref=field, send_sem=state_send.at[way], recv_sem=state_recv,
            device_id={"tm": to},
        )

    def partner_copy(slot):
        return pltpu.make_async_remote_copy(
            src_ref=edge_out.at[slot + 1, 0], dst_ref=from_partner.at[slot],
            send_sem=partner_send.at[slot], recv_sem=partner_recv.at[slot],
            device_id={"space": partner},
        )

    def second_copy(slot, to):
        return pltpu.make_async_remote_copy(
            src_ref=edge_out.at[slot + 1, 0], dst_ref=from_second.at[slot + 1],
            send_sem=second_send.at[slot + 1], recv_sem=second_recv.at[slot + 1],
            device_id={"space": to},
        )

    def across_copy(slot):
        return pltpu.make_async_remote_copy(
            src_ref=part_out.at[slot], dst_ref=from_across.at[slot],
            send_sem=across_send.at[slot], recv_sem=across_recv.at[slot],
            device_id={"space": across},
        )

    def first_copies(slot, way, to):
        kinds = ((0, partner, from_partner.at[0], partner_recv.at[0]),
                 (1, across, from_across.at[0], across_recv.at[0]),
                 (0, beyond, from_second.at[1], second_recv.at[1]))
        return [
            pltpu.make_async_remote_copy(
                src_ref=edge_out.at[slot + 1, side], dst_ref=ref,
                send_sem=first_send.at[way, i], recv_sem=recv,
                device_id={"tm": to, "space": place},
            )
            for i, (side, place, ref, recv) in enumerate(kinds)
        ]

    def first_send_all(slot, way, to):
        near_one, across_one, second_one = first_copies(slot, way, to)

        @pl.when(has_across)
        def _():
            across_one.start()

        @pl.when(has_beyond)
        def _():
            second_one.start()

        near_one.start()

    def first_drain(slot, way, to):
        near_one, across_one, second_one = first_copies(slot, way, to)

        @pl.when(has_across)
        def _():
            across_one.wait_send()

        @pl.when(has_beyond)
        def _():
            second_one.wait_send()

        near_one.wait_send()

    def choose(slot):
        values = matmul(select_terms[...], field_terms[...])
        for side in range(2):
            for j in range(comp):
                edge_out[slot + 1, side, j] = values[side * count : (side + 1) * count, lanes(j)]

    @pl.when(g == top)
    def _():
        for t in range(tiles):
            r = rows_at(t * TILE)
            for j in range(comp):
                x = live_of(t) * terminal[j, r, :]
                field[j, r, :] = x
                put_terms(field_terms, t, j, x)
        choose(-1)
        first_send_all(-1, 0, g)

    @pl.when(has_across)
    def _():
        fixed_copy().start()
        rate_copy(0).start()

    @pl.when(twice)
    def _():
        jac_copy(g).wait_recv()
        for t in range(tiles):
            prepare(t, 1)
        for j in range(comp):
            own_rate[1, j] = matmul(chosen, rate[1, j], HIGHEST)

        @pl.when(has_across)
        def _():
            rate_copy(1).start()

    @pl.when(g < top)
    def _():
        state_copy(0, g).wait_recv()
        for t in range(tiles):
            for j in range(comp):
                put_terms(field_terms, t, j, field[j, rows_at(t * TILE), :])

    def sweep(m):
        store = jnp.where(twice & (m < sweeps), 1, 0)
        choose(m)

        @pl.when(m > 0)
        def _():
            partner_copy(m).start()

            @pl.when(has_beyond & (m < last - 1))
            def _():
                second_copy(m, beyond).start()

        near[...] = matmul(near_pick[...], field_terms[...])

        for t in range(tiles):
            r = rows_at(t * TILE)
            x = [field[i, r, :] for i in range(comp)]
            left = cell_left[r, :]
            right = cell_right[r, :]
            for j in range(comp):
                value = left * pltpu.roll(x[j], 1, 1) + right * pltpu.roll(x[j], cells - 1, 1)
                for k in range(nei):
                    q = rows_at(k * nb + t * TILE)
                    value = value + face[k, r, :] * near[q, lanes(j)]
                value = rhs[j, r, :] + rate[store, j, r, :] * value
                for i in range(comp):
                    value = value + jac[store, i, j, r, :] * x[i]
                part[j, r, :] = value
                put_terms(part_terms, t, j, value)

        @pl.when(has_across & (m < last - 1))
        def _():
            ahead = matmul(select_terms[count:edges, :], part_terms[...])
            for j in range(comp):
                part_out[m + 1, j] = ahead[:, lanes(j)]
            across_copy(m + 1).start()

        @pl.when(has_across & (m == 1))
        def _():
            fixed_copy().wait_recv()
            rate_copy(0).wait_recv()
            for k in range(nei):
                their_pick[k * count : (k + 1) * count, :] = their_fixed[k].astype(jnp.bfloat16)

            @pl.when(twice)
            def _():
                rate_copy(1).wait_recv()

        @pl.when(has_across & (m > 0))
        def _():
            kept = jnp.where(twice & (m <= sweeps), 1, 0)
            second_copy(m - 1, second).wait_recv()
            for side in range(2):
                for j in range(comp):
                    put_edges(edge_terms, side, j, from_second[m, j] if side == 0 else edge_out[m, 1, j])
            arrived = matmul(their_pick[...], edge_terms[...])
            for j in range(comp):
                value = None
                for k in range(nei):
                    term = their_fixed[nei + k] * arrived[k * count : (k + 1) * count, lanes(j)]
                    value = term if value is None else value + term
                edge_halo[j] = their_rate[kept, j] * value

        partner_copy(m).wait_recv()
        for j in range(comp):
            put_edges(halo_terms, 0, j, from_partner[m, j])

        @pl.when(has_across)
        def _():
            across_copy(m).wait_recv()

        for j in range(comp):
            put_edges(halo_terms, 1, j, from_across[m, j] + edge_halo[j])

        far[...] = matmul(far_pick[...], halo_terms[...])

        for t in range(tiles):
            r = rows_at(t * TILE)
            for j in range(comp):
                value = None
                for k in range(nei):
                    q = rows_at(k * nb + t * TILE)
                    term = face[k, r, :] * far[q, lanes(j)]
                    value = term if value is None else value + term
                value = part[j, r, :] + rate[store, j, r, :] * value
                field[j, r, :] = value
                put_terms(field_terms, t, j, value)

    def level_copy(n):
        return pltpu.make_async_copy(levels.at[n], adjoint_hbm.at[n], store_sem.at[n])

    def level(step, _):
        copied = twice & (step < steps)
        store = jnp.where(copied, 1, 0)
        n = steps - 1 - lax.rem(step, steps)

        @pl.when(copied)
        def _():
            source_copy(n, g).wait_recv()

        for t in range(tiles):
            r = rows_at(t * TILE)
            for j in range(comp):
                rhs[j, r, :] = (
                    rate[store, j, r, :] * source[store, n, j, r, :] + rate_mass[store, j, r, :] * field[j, r, :]
                )

        def one(it, _):
            sweep(step * ITERS + it)
            return 0

        lax.fori_loop(0, ITERS, one, 0)

        @pl.when((step == stages * steps - 1) & down_one)
        def _():
            @pl.when(down_two)
            def _():
                state_copy(0, g - 2).start()

            choose(last)

            @pl.when(down_two)
            def _():
                first_send_all(last, 0, g - 2)

            state_copy(1, g - 1).start()
            first_send_all(last, 1, g - 1)

        @pl.when(jnp.logical_not(copied))
        def _():
            weight = weights[n]
            for t in range(tiles):
                r = rows_at(t * TILE)
                for j in range(comp):
                    x = field[j, r, :]
                    levels[n, j, r, :] = x
                    weighted[j, r, :] = weighted[j, r, :] + weight * x
            level_copy(n).start()

        return 0

    def level_if(step, _):
        @pl.when(step < stages * steps)
        def _():
            level(step, 0)

        return 0

    lax.fori_loop(0, 2 * steps, level_if, 0)

    summed = jnp.zeros((nb, cells), jnp.float32)
    for j in range(comp):
        summed = summed + weighted[j] * shape[j]

    mine = lax.dot_general(
        jnp.ones((8, cells), jnp.float32),
        summed,
        (((1,), (1,)), ((), ())),
        precision=lax.Precision.HIGHEST,
        preferred_element_type=jnp.float32,
    )

    def acc_copy(to):
        return pltpu.make_async_remote_copy(
            src_ref=acc_out, dst_ref=acc_in, send_sem=acc_send, recv_sem=acc_recv,
            device_id={"tm": to},
        )

    def total_copy(to):
        return pltpu.make_async_remote_copy(
            src_ref=acc_out, dst_ref=total, send_sem=total_send.at[to], recv_sem=total_recv,
            device_id={"tm": to},
        )

    @pl.when(g == top)
    def _():
        acc_out[...] = mine

    @pl.when(g < top)
    def _():
        acc_copy(g).wait_recv()
        acc_out[...] = mine + acc_in[...]

    @pl.when(g > 0)
    def _():
        acc_copy(g - 1).start()
        total_copy(g).wait_recv()
        sens_ref[...] = total[0:1, :]

    @pl.when(g == 0)
    def _():
        for other in range(1, groups):
            total_copy(other).start()
        sens_ref[...] = acc_out[0:1, :]
        for other in range(1, groups):
            total_copy(other).wait_send()

    @pl.when(g > 0)
    def _():
        acc_copy(g - 1).wait_send()

    @pl.when(copies)
    def _():
        jac_copy(g - 1).wait_send()
        for n in range(steps):
            source_copy(n, g - 1).wait_send()

    @pl.when(has_across)
    def _():
        fixed_copy().wait_send()
        rate_copy(0).wait_send()

        @pl.when(twice)
        def _():
            rate_copy(1).wait_send()

    @pl.when(g == top)
    def _():
        first_drain(-1, 0, g)

    @pl.when(down_two)
    def _():
        state_copy(0, g - 2).wait_send()
        first_drain(last, 0, g - 2)

    @pl.when(down_one)
    def _():
        state_copy(1, g - 1).wait_send()
        first_drain(last, 1, g - 1)

    def drain(slot, _):
        @pl.when(slot < last)
        def _():
            partner_copy(slot).wait_send()

        @pl.when(has_beyond & (slot < last - 1))
        def _():
            second_copy(slot, beyond).wait_send()

        @pl.when(has_across & (slot < last))
        def _():
            across_copy(slot).wait_send()

        return 0

    lax.fori_loop(1, 2 * sweeps, drain, 0)
    for n in range(steps):
        level_copy(n).wait()


def per_device(groups, width, *args):
    (source, terminal, jacobian, face_coef, cell_coef, neighbours, send_blocks,
     live_count, volume, shape_field, weights) = args
    steps, nb, comp, cells = source.shape
    nei = face_coef.shape[1]
    count = send_blocks.shape[2]
    edges = 2 * count
    slots = 2 * steps * ITERS
    f32 = jnp.float32
    bf16 = jnp.bfloat16
    hbm = pl.BlockSpec(memory_space=pltpu.MemorySpace.HBM)
    smem = pl.BlockSpec(memory_space=pltpu.SMEM)
    vmem = pltpu.VMEM
    dma = pltpu.SemaphoreType.DMA
    block = (comp, nb, cells)
    flat = comp * cells
    edge = (comp, count, cells)
    adjoint, sens = pl.pallas_call(
        functools.partial(kernel, groups, width),
        out_shape=(
            jax.ShapeDtypeStruct((steps, comp, nb, cells), f32),
            jax.ShapeDtypeStruct((1, nb), f32),
        ),
        in_specs=[hbm, hbm, hbm, hbm, hbm, hbm, smem, smem, hbm, hbm, smem],
        out_specs=(hbm, pl.BlockSpec(memory_space=pltpu.VMEM)),
        scratch_shapes=[
            vmem((2, steps, comp, nb, cells), f32),
            vmem(block, f32),
            vmem((2, comp, comp, nb, cells), f32),
            vmem((nei, nb, cells), f32),
            vmem((nb, cells), f32),
            vmem((nei, nb), jnp.int32),
            vmem((nb, cells), f32),
            vmem(block, f32),
            vmem(block, f32),
            vmem(block, f32),
            vmem((2,) + block, f32),
            vmem((2,) + block, f32),
            vmem((nb, cells), f32),
            vmem((nb, cells), f32),
            vmem(block, f32),
            vmem((steps, comp, nb, cells), f32),
            vmem(block, f32),
            vmem((nei * nb, 2 * nb), bf16),
            vmem((nei * nb, nb), bf16),
            vmem((2 * nb, flat), bf16),
            vmem((2 * nb, flat), bf16),
            vmem((nb, flat), bf16),
            vmem((nb, flat), bf16),
            vmem((nei * nb, flat), f32),
            vmem((nei * nb, flat), f32),
            vmem((edges, nb), f32),
            vmem((edges, 2 * nb), bf16),
            vmem((2 * nei, count, cells), f32),
            vmem((2,) + edge, f32),
            vmem((2 * nei, count, cells), f32),
            vmem((2,) + edge, f32),
            vmem((nei * count, nb), bf16),
            vmem(edge, f32),
            vmem((slots + 1,) + edge, f32),
            vmem((slots + 1,) + edge, f32),
            vmem((slots + 1,) + edge, f32),
            vmem((slots + 2, 2) + edge, f32),
            vmem((slots + 1,) + edge, f32),
            vmem((8, nb), f32),
            vmem((8, nb), f32),
            vmem((8, nb), f32),
            dma((8,)),
            dma((steps,)),
            dma((1 + steps,)),
            dma((1 + steps,)),
            dma((3,)),
            dma((3,)),
            dma((slots + 1,)),
            dma((slots + 1,)),
            dma((slots + 1,)),
            dma((slots + 1,)),
            dma((slots + 1,)),
            dma((slots + 1,)),
            dma((2, 3)),
            dma((2,)),
            dma,
            dma,
            dma,
            dma((groups,)),
            dma,
        ],
        compiler_params=pltpu.CompilerParams(collective_id=0, has_side_effects=True),
    )(
        source.transpose(0, 2, 1, 3),
        terminal.transpose(1, 0, 2),
        jacobian.transpose(0, 2, 3, 1, 4),
        face_coef.transpose(1, 0, 2),
        cell_coef,
        neighbours.T,
        send_blocks,
        live_count,
        volume,
        shape_field.transpose(1, 0, 2),
        weights,
    )
    return adjoint.transpose(0, 2, 1, 3), sens.reshape(nb)


def solution(mesh):
    sizes = dict(mesh.shape)
    return jax.shard_map(
        functools.partial(per_device, sizes["tm"], sizes["space"]),
        mesh=mesh,
        in_specs=(
            P("tm", "space", None, None),
            P("space", None, None),
            P("tm", "space", None, None, None),
            P("space", None, None),
            P("space", None),
            P("space", None),
            P("space", None, None),
            P("space"),
            P("space", None),
            P("space", None, None),
            P("tm"),
        ),
        out_specs=(P("tm", "space", None, None), P("space")),
        check_vma=False,
    )
```

time: 103 us -> 87.9 us (0.85); the launches traced: 101 us -> 87.7 us
  Pallas kernels: 97 us -> 83.2 us
    pallas_call x1, Pallas kernels: 97 us -> 83.2 us  [per_device(): pl.pallas_call(functools.partial(kernel, groups, width), out_shape=(jax.S...]
where the time goes in v1:
time: 87.9 us; the launch traced here: 87.7 us
  Pallas kernels  83.2 us (95%)
  local copies, waits for them, and re-layouts  3.14 us (4%)
  between operations  1.29 us (1%)
    pallas_call x1, Pallas kernels, per_device(): pl.pallas_call(functools.partial(kernel, groups, width), out_shape=(jax.S...  83.2 us
    unnamed x2, local copies, waits for them, and re-layouts  3.14 us

profile of v1, /device:TPU:0, one launch (start us, length us, event | category | flops | bytes accessed | tf_op | source)
XLA Modules:
  0.0 87.7 jit_solution(9484681179907908508)
XLA Ops:
  1.3 83.2 %shard_map.122 = (f32[2,5,128,128]{3,2,1,0:T(8,128)}, f32[1,128]{1,0:T(1,128)}) custom-call(f32[2,5,128,128]{3,2,1,0:T(8,128)} %bitcast.10, f32[5,128,128]{2,1,0:T(8,128)} %bitcast.12, f32[1,5,5,128,128]{4,3,2,1,0:T(8,128)} %bitcast.8, f32[6,128,128]{2,1,0:T(8,128)} %bitcast.11, f32[128,128]{1,0:T(8,128)} %cell_hbm.1, s32[6,128]{1,0:T(8,128)} %bitcast.14, ...), custom_call_target="tpu_custom_call" | custom-call | tf_op jit(solution)/shard_map/pallas_call | solution.py:674
  84.5 2.0 %copy.16 = f32[2,128,5,128]{3,1,2,0:T(8,128)} copy(f32[2,128,5,128]{3,1,2,0:T(8,128)} %bitcast.9) | data formatting | bytes 1310720
  86.5 1.2 %copy.17 = f32[128]{0:T(128)} copy(f32[128]{0:T(128)} %bitcast.15) | data formatting | bytes 1024

commit v2 on v1

--- a/solution.py
+++ b/solution.py
@@ -10,7 +10,6 @@
 ITERS = 3
 INVERSE_STEP = 6.0
 TILE = 16
-HIGHEST = lax.Precision.HIGHEST
 
 
 def rows_at(start):
@@ -22,8 +21,8 @@
     return high, (x - high.astype(jnp.float32)).astype(jnp.bfloat16)
 
 
-def matmul(a, b, precision=None):
-    return jnp.dot(a, b, precision=precision, preferred_element_type=jnp.float32)
+def matmul(a, b):
+    return jnp.dot(a, b, preferred_element_type=jnp.float32)
 
 
 def kernel(
@@ -62,13 +61,11 @@
     near_pick,
     far_pick,
     field_terms,
-    part_terms,
     halo_terms,
     edge_terms,
     near,
     far,
     select,
-    select_terms,
     own_fixed,
     own_rate,
     their_fixed,
@@ -194,20 +191,16 @@
         for n in reversed(range(steps)):
             source_copy(n, g - 1).start()
 
+    def block_of(side, s):
+        return jnp.where(odd == side, send_blocks[0, 1, s], send_blocks[0, 0, s])
+
     halo_terms[...] = jnp.zeros_like(halo_terms)
     edge_terms[...] = jnp.zeros_like(edge_terms)
     edge_halo[...] = jnp.zeros_like(edge_halo)
     lane = lax.broadcasted_iota(jnp.int32, (1, nb), 1)
-    for i in range(2):
-        for s in range(count):
-            row = i * count + s
-            block = jnp.where(odd == i, send_blocks[0, 1, s], send_blocks[0, 0, s])
-            select[pl.ds(row, 1), :] = jnp.where(lane == block, 1.0, 0.0)
-    chosen_low = select[...].astype(jnp.bfloat16)
-    select_terms[:, :nb] = chosen_low
-    select_terms[:, nb:] = chosen_low
-    chosen = select[count:edges, :]
-    chosen_low = chosen.astype(jnp.bfloat16)
+    for s in range(count):
+        select[pl.ds(s, 1), :] = jnp.where(lane == block_of(1, s), 1.0, 0.0)
+    chosen = select[...].astype(jnp.bfloat16)
 
     loads[0].wait()
     listed = nbr[...].astype(jnp.float32)
@@ -225,7 +218,7 @@
         hit = (shifted == wide) | (shifted + edges == wide)
         pick = jnp.where(hit & inside, 1.0, 0.0).astype(jnp.bfloat16)
         far_pick[pl.ds(k * nb, nb), :] = pick
-        own_fixed[k] = matmul(chosen_low, pick)
+        own_fixed[k] = matmul(chosen, pick)
 
     for load in loads[1:5]:
         load.wait()
@@ -272,10 +265,12 @@
 
     for t in range(tiles):
         prepare(t, 0)
-    for k in range(nei):
-        own_fixed[nei + k] = matmul(chosen, face[k], HIGHEST)
-    for j in range(comp):
-        own_rate[0, j] = matmul(chosen, rate[0, j], HIGHEST)
+    for s in range(count):
+        block = pl.ds(block_of(1, s), 1)
+        for k in range(nei):
+            own_fixed[nei + k, pl.ds(s, 1), :] = face[k, block, :]
+        for j in range(comp):
+            own_rate[0, j, pl.ds(s, 1), :] = rate[0, j, block, :]
 
     for load in loads[5:]:
         load.wait()
@@ -363,11 +358,10 @@
 
         near_one.wait_send()
 
-    def choose(slot):
-        values = matmul(select_terms[...], field_terms[...])
-        for side in range(2):
+    def choose(slot, side):
+        for s in range(count):
             for j in range(comp):
-                edge_out[slot + 1, side, j] = values[side * count : (side + 1) * count, lanes(j)]
+                edge_out[slot + 1, side, j, pl.ds(s, 1), :] = field[j, pl.ds(block_of(side, s), 1), :]
 
     @pl.when(g == top)
     def _():
@@ -377,7 +371,8 @@
                 x = live_of(t) * terminal[j, r, :]
                 field[j, r, :] = x
                 put_terms(field_terms, t, j, x)
-        choose(-1)
+        for side in range(2):
+            choose(-1, side)
         first_send_all(-1, 0, g)
 
     @pl.when(has_across)
@@ -390,8 +385,9 @@
         jac_copy(g).wait_recv()
         for t in range(tiles):
             prepare(t, 1)
-        for j in range(comp):
-            own_rate[1, j] = matmul(chosen, rate[1, j], HIGHEST)
+        for s in range(count):
+            for j in range(comp):
+                own_rate[1, j, pl.ds(s, 1), :] = rate[1, j, pl.ds(block_of(1, s), 1), :]
 
         @pl.when(has_across)
         def _():
@@ -406,7 +402,7 @@
 
     def sweep(m):
         store = jnp.where(twice & (m < sweeps), 1, 0)
-        choose(m)
+        choose(m, 0)
 
         @pl.when(m > 0)
         def _():
@@ -416,6 +412,7 @@
             def _():
                 second_copy(m, beyond).start()
 
+        choose(m, 1)
         near[...] = matmul(near_pick[...], field_terms[...])
 
         for t in range(tiles):
@@ -432,13 +429,12 @@
                 for i in range(comp):
                     value = value + jac[store, i, j, r, :] * x[i]
                 part[j, r, :] = value
-                put_terms(part_terms, t, j, value)
 
         @pl.when(has_across & (m < last - 1))
         def _():
-            ahead = matmul(select_terms[count:edges, :], part_terms[...])
-            for j in range(comp):
-                part_out[m + 1, j] = ahead[:, lanes(j)]
+            for s in range(count):
+                for j in range(comp):
+                    part_out[m + 1, j, pl.ds(s, 1), :] = part[j, pl.ds(block_of(1, s), 1), :]
             across_copy(m + 1).start()
 
         @pl.when(has_across & (m == 1))
@@ -523,7 +519,8 @@
             def _():
                 state_copy(0, g - 2).start()
 
-            choose(last)
+            for side in range(2):
+                choose(last, side)
 
             @pl.when(down_two)
             def _():
@@ -700,13 +697,11 @@
             vmem((nei * nb, 2 * nb), bf16),
             vmem((nei * nb, nb), bf16),
             vmem((2 * nb, flat), bf16),
-            vmem((2 * nb, flat), bf16),
             vmem((nb, flat), bf16),
             vmem((nb, flat), bf16),
             vmem((nei * nb, flat), f32),
             vmem((nei * nb, flat), f32),
-            vmem((edges, nb), f32),
-            vmem((edges, 2 * nb), bf16),
+            vmem((count, nb), f32),
             vmem((2 * nei, count, cells), f32),
             vmem((2,) + edge, f32),
             vmem((2 * nei, count, cells), f32),

time: 87.9 us -> 84.4 us (0.960)
  Pallas kernels: 83.2 us -> 79.7 us
    pallas_call x1, Pallas kernels: 83.2 us -> 79.7 us  [per_device(): pl.pallas_call(functools.partial(kernel, groups, width), out_shape=(jax.S...]
where the time goes in v2:
time: 84.4 us; the launch traced here: 84.2 us
  Pallas kernels  79.7 us (94%)
  local copies, waits for them, and re-layouts  3.14 us (4%)
  between operations  1.29 us (2%)
    pallas_call x1, Pallas kernels, per_device(): pl.pallas_call(functools.partial(kernel, groups, width), out_shape=(jax.S...  79.7 us
    unnamed x2, local copies, waits for them, and re-layouts  3.14 us

profile of v2, /device:TPU:0, one launch (start us, length us, event | category | flops | bytes accessed | tf_op | source)
XLA Modules:
  0.0 84.2 jit_solution(15203188522576205454)
XLA Ops:
  1.3 79.7 %shard_map.122 = (f32[2,5,128,128]{3,2,1,0:T(8,128)}, f32[1,128]{1,0:T(1,128)}) custom-call(f32[2,5,128,128]{3,2,1,0:T(8,128)} %bitcast.10, f32[5,128,128]{2,1,0:T(8,128)} %bitcast.12, f32[1,5,5,128,128]{4,3,2,1,0:T(8,128)} %bitcast.8, f32[6,128,128]{2,1,0:T(8,128)} %bitcast.11, f32[128,128]{1,0:T(8,128)} %cell_hbm.1, s32[6,128]{1,0:T(8,128)} %bitcast.14, ...), custom_call_target="tpu_custom_call" | custom-call | tf_op jit(solution)/shard_map/pallas_call | solution.py:671
  81.0 2.0 %copy.16 = f32[2,128,5,128]{3,1,2,0:T(8,128)} copy(f32[2,128,5,128]{3,1,2,0:T(8,128)} %bitcast.9) | data formatting | bytes 1310720
  83.0 1.2 %copy.17 = f32[128]{0:T(128)} copy(f32[128]{0:T(128)} %bitcast.15) | data formatting | bytes 1024

commit v3 on v2

--- a/solution.py
+++ b/solution.py
@@ -402,17 +402,6 @@
 
     def sweep(m):
         store = jnp.where(twice & (m < sweeps), 1, 0)
-        choose(m, 0)
-
-        @pl.when(m > 0)
-        def _():
-            partner_copy(m).start()
-
-            @pl.when(has_beyond & (m < last - 1))
-            def _():
-                second_copy(m, beyond).start()
-
-        choose(m, 1)
         near[...] = matmul(near_pick[...], field_terms[...])
 
         for t in range(tiles):
@@ -437,6 +426,8 @@
                     part_out[m + 1, j, pl.ds(s, 1), :] = part[j, pl.ds(block_of(1, s), 1), :]
             across_copy(m + 1).start()
 
+        choose(m, 1)
+
         @pl.when(has_across & (m == 1))
         def _():
             fixed_copy().wait_recv()
@@ -478,15 +469,25 @@
 
         for t in range(tiles):
             r = rows_at(t * TILE)
+            faces = [face[k, r, :] for k in range(nei)]
             for j in range(comp):
                 value = None
                 for k in range(nei):
                     q = rows_at(k * nb + t * TILE)
-                    term = face[k, r, :] * far[q, lanes(j)]
+                    term = faces[k] * far[q, lanes(j)]
                     value = term if value is None else value + term
                 value = part[j, r, :] + rate[store, j, r, :] * value
                 field[j, r, :] = value
                 put_terms(field_terms, t, j, value)
+
+        @pl.when(m < last - 1)
+        def _():
+            choose(m + 1, 0)
+            partner_copy(m + 1).start()
+
+            @pl.when(has_beyond & (m < last - 2))
+            def _():
+                second_copy(m + 1, beyond).start()
 
     def level_copy(n):
         return pltpu.make_async_copy(levels.at[n], adjoint_hbm.at[n], store_sem.at[n])
@@ -708,11 +709,11 @@
             vmem((2,) + edge, f32),
             vmem((nei * count, nb), bf16),
             vmem(edge, f32),
-            vmem((slots + 1,) + edge, f32),
-            vmem((slots + 1,) + edge, f32),
-            vmem((slots + 1,) + edge, f32),
+            vmem((slots + 2,) + edge, f32),
+            vmem((slots + 2,) + edge, f32),
+            vmem((slots + 2,) + edge, f32),
             vmem((slots + 2, 2) + edge, f32),
-            vmem((slots + 1,) + edge, f32),
+            vmem((slots + 2,) + edge, f32),
             vmem((8, nb), f32),
             vmem((8, nb), f32),
             vmem((8, nb), f32),
@@ -722,12 +723,12 @@
             dma((1 + steps,)),
             dma((3,)),
             dma((3,)),
-            dma((slots + 1,)),
-            dma((slots + 1,)),
-            dma((slots + 1,)),
-            dma((slots + 1,)),
-            dma((slots + 1,)),
-            dma((slots + 1,)),
+            dma((slots + 2,)),
+            dma((slots + 2,)),
+            dma((slots + 2,)),
+            dma((slots + 2,)),
+            dma((slots + 2,)),
+            dma((slots + 2,)),
             dma((2, 3)),
             dma((2,)),
             dma,

time: 84.4 us -> 84.2 us (level)
  no operation moved by 1% of the time
where the time goes in v3:
time: 84.2 us; the launch traced here: 84 us
  Pallas kernels  79.6 us (95%)
  local copies, waits for them, and re-layouts  3.14 us (4%)
  between operations  1.29 us (2%)
    pallas_call x1, Pallas kernels, per_device(): pl.pallas_call(functools.partial(kernel, groups, width), out_shape=(jax.S...  79.6 us
    unnamed x2, local copies, waits for them, and re-layouts  3.14 us

profile of v3, /device:TPU:0, one launch (start us, length us, event | category | flops | bytes accessed | tf_op | source)
XLA Modules:
  0.0 84.0 jit_solution(6571537392655877)
XLA Ops:
  1.3 79.6 %shard_map.122 = (f32[2,5,128,128]{3,2,1,0:T(8,128)}, f32[1,128]{1,0:T(1,128)}) custom-call(f32[2,5,128,128]{3,2,1,0:T(8,128)} %bitcast.10, f32[5,128,128]{2,1,0:T(8,128)} %bitcast.12, f32[1,5,5,128,128]{4,3,2,1,0:T(8,128)} %bitcast.8, f32[6,128,128]{2,1,0:T(8,128)} %bitcast.11, f32[128,128]{1,0:T(8,128)} %cell_hbm.1, s32[6,128]{1,0:T(8,128)} %bitcast.14, ...), custom_call_target="tpu_custom_call" | custom-call | tf_op jit(solution)/shard_map/pallas_call | solution.py:672
  80.8 2.0 %copy.16 = f32[2,128,5,128]{3,1,2,0:T(8,128)} copy(f32[2,128,5,128]{3,1,2,0:T(8,128)} %bitcast.9) | data formatting | bytes 1310720
  82.8 1.2 %copy.17 = f32[128]{0:T(128)} copy(f32[128]{0:T(128)} %bitcast.15) | data formatting | bytes 1024
